TPU v7x, 32 devices: a whole 2x2x4 slice. The times are simulated.
32 devices in a mesh: blk: 8 (over z, x), rows: 4 (over y, core).
Axes of the slice: x: 2, y: 2, z: 4, core: 2. Of those that a mesh axis runs over, the one named last changes fastest.
Arguments:
- centers: int32 [512, 1], P(('blk', 'rows')), may hold values from 0 to 127, as said below
- gates_used: int32 [512], P(('blk', 'rows')), may hold values from 12 to 40
- jacobian: bfloat16 [512, 3, 40, 256], P(('blk', 'rows')), may hold values from -0.3984375 to 0.3984375
- weights: bfloat16 [512, 40], P(('blk', 'rows')), may hold values from 0.099609375 to 1
Outputs:
- hessian_band: float32 [128, 3, 256, 256], P(('blk', 'rows'))
Inputs may be any that keep to these rules, and one draw needn't show every extreme that they name: `centers`: cell block c is owned by blk index c // 16. Among the soundings of one device at most 4 are centred on blocks of one owner, and some owner gets exactly 4 of them; the number a device sends to the owner k places further along blk (cyclically) is the same for all devices of one rows index. Among the soundings of all devices of one rows index at most 2 share a centre block, and some block has exactly 2.
All inputs are finite; a program needn't handle non-finite values.
Results may differ from a plain program's by a relative error of at most 0.0024.
Values may be sent and summed in bfloat16 or wider, within the bound.
No kernel may reach another device: no remote copies, remote signals or barrier semaphores. Data moves between devices by JAX's collectives and lax.ppermute only.
A program may use at most 128 MiB of HBM per device.

v0:
```python
import jax
import jax.numpy as jnp
from jax import lax
from jax.sharding import PartitionSpec as P

KB = 16


def with_halo(block, sides, width):
    for axis, dim in sides:
        count = lax.axis_size(axis)
        forward = [(i, i + 1) for i in range(count - 1)]
        backward = [(target, source) for source, target in forward]
        low = lax.ppermute(
            lax.slice_in_dim(block, block.shape[dim] - width, None, axis=dim), axis, forward
        )
        high = lax.ppermute(lax.slice_in_dim(block, 0, width, axis=dim), axis, backward)
        block = jnp.concatenate([low, block, high], axis=dim)
    return block


def rank_among(labels):
    positions = jnp.arange(labels.shape[0], dtype=jnp.int32)
    before = (labels[None, :] == labels[:, None]) & (positions[None, :] < positions[:, None])
    return jnp.sum(before.astype(jnp.int32), axis=1)


def band_terms(buckets, bucket_wts, base, total_blocks):
    block_num, slot_len, foot_len, gate_len, cell_len = buckets.shape
    grid_pos = (
        base
        + jnp.arange(block_num, dtype=jnp.int32)[:, None]
        + jnp.arange(foot_len, dtype=jnp.int32)[None, :]
        - 1
    )
    inside = ((grid_pos >= 0) & (grid_pos < total_blocks)).astype(jnp.float32)
    scaled = (
        buckets.astype(jnp.float32)
        * bucket_wts.astype(jnp.float32)[:, :, None, :, None]
        * inside[:, None, :, None, None]
    ).astype(jnp.bfloat16)
    masked = buckets * inside.astype(jnp.bfloat16)[:, None, :, None, None]
    accum = jnp.zeros((block_num + 2, foot_len, cell_len, cell_len), jnp.float32)
    for lead_pos in range(foot_len):
        left = scaled[:, :, lead_pos].reshape(block_num, slot_len * gate_len, cell_len)
        for offset in range(foot_len - lead_pos):
            right = masked[:, :, lead_pos + offset].reshape(
                block_num, slot_len * gate_len, cell_len
            )
            term = lax.dot_general(
                left, right, (((1,), (1,)), ((0,), (0,))), preferred_element_type=jnp.float32
            )
            accum = accum.at[lead_pos : lead_pos + block_num, offset].add(term)
    return accum


def edge_rows(accum):
    return jnp.stack([accum[0], accum[accum.shape[0] - 1]])


def attach(accum, padded):
    block_num = accum.shape[0] - 2
    core = accum[1 : block_num + 1]
    core = core.at[0].add(padded[0])
    return core.at[block_num - 1].add(padded[3])


def on_device(centers, gates_used, jacobian, weights):
    blk_count = lax.axis_size("blk")
    sound_count, foot_len, gate_len, cell_len = jacobian.shape
    capacity = max(2, 2 * sound_count // blk_count)
    bucket_cap = max(2, 2 * sound_count // KB)
    slot_count = blk_count * capacity
    total_blocks = blk_count * KB
    centre_ids = centers[:, 0]
    owner = centre_ids // KB
    within = centre_ids - owner * KB
    order_in = rank_among(owner)
    gate_live = jnp.arange(gate_len, dtype=jnp.int32)[None, :] < gates_used[:, None]
    weight_live = jnp.where(gate_live, weights, jnp.zeros_like(weights))
    target = owner * capacity + order_in
    select = (target[None, :] == jnp.arange(slot_count, dtype=jnp.int32)[:, None]).astype(
        jnp.bfloat16
    )
    packed = (
        jnp.dot(select, jacobian.reshape(sound_count, -1), preferred_element_type=jnp.float32)
        .astype(jnp.bfloat16)
        .reshape(slot_count, foot_len, gate_len, cell_len)
    )
    packed_wts = jnp.dot(select, weight_live, preferred_element_type=jnp.float32).astype(
        jnp.bfloat16
    )
    packed_ids = jnp.dot(
        select, (within + 1).astype(jnp.bfloat16)[:, None], preferred_element_type=jnp.float32
    ).astype(jnp.bfloat16)[:, 0]
    received, received_wts, received_ids = (
        lax.all_to_all(packed, "blk", split_axis=0, concat_axis=0, tiled=True),
        lax.all_to_all(packed_wts, "blk", split_axis=0, concat_axis=0, tiled=True),
        lax.all_to_all(packed_ids, "blk", split_axis=0, concat_axis=0, tiled=True),
    )
    arrived_ids = received_ids.astype(jnp.int32)
    arrived_rank = rank_among(arrived_ids)
    bucket_target = jnp.where(arrived_ids > 0, (arrived_ids - 1) * bucket_cap + arrived_rank, -1)
    bucket_count = KB * bucket_cap
    bucket_sel = (
        bucket_target[None, :] == jnp.arange(bucket_count, dtype=jnp.int32)[:, None]
    ).astype(jnp.bfloat16)
    buckets = (
        jnp.dot(bucket_sel, received.reshape(slot_count, -1), preferred_element_type=jnp.float32)
        .astype(jnp.bfloat16)
        .reshape(KB, bucket_cap, foot_len, gate_len, cell_len)
    )
    bucket_wts = (
        jnp.dot(bucket_sel, received_wts, preferred_element_type=jnp.float32)
        .astype(jnp.bfloat16)
        .reshape(KB, bucket_cap, gate_len)
    )
    mine_blk = lax.axis_index("blk")
    share = KB // lax.axis_size("rows")
    moved, moved_wts = (
        lax.all_to_all(buckets, "rows", split_axis=0, concat_axis=1, tiled=True),
        lax.all_to_all(bucket_wts, "rows", split_axis=0, concat_axis=1, tiled=True),
    )
    base = mine_blk * KB + lax.axis_index("rows") * share
    accum = band_terms(moved, moved_wts, base, total_blocks)
    padded = with_halo(edge_rows(accum), ((("blk", "rows"), 0),), 1)
    return attach(accum, padded)


def solution(mesh):
    placed = (
        P(("blk", "rows"), None),
        P(("blk", "rows")),
        P(("blk", "rows"), None, None, None),
        P(("blk", "rows"), None),
    )
    return jax.shard_map(
        on_device,
        mesh=mesh,
        in_specs=placed,
        out_specs=P(("blk", "rows"), None, None, None),
        check_vma=False,
    )
```

profile of v0, /device:TPU:3, one launch (start us, length us, event | category | flops | bytes accessed | tf_op | source)
XLA Modules:
  0.0 140.4 jit_solution(17639520557241093231)
XLA Ops:
  0.0 0.7 and_select_fusion.1
  0.7 0.7 fusion.55
  1.3 0.2 convert_reduce_fusion.1
  1.5 0.7 multiply_add_fusion
  2.2 0.8 fusion.9
  3.0 0.7 all_to_all.48
  3.6 5.8 %all-to-all-start = ((bf16[8,4,1]{1,2,0:T(2,128)(2,1)}), bf16[8,4,1]{1,2,0:T(2,128)(2,1)S(1)}, u32[]{:S(2)}, u32[]{:S(2)}) async-start(bf16[8,4,1]{1,2,0:T(2,128)(2,1)} %all_to_all.48), calls=%async_computation | async-start | bytes 8192 | tf_op jit(solution)/shard_map/all_to_all | solution.py:99
  9.4 1.5 %convolution_convert_fusion.3 = bf16[32,40]{1,0:T(8,128)(2,1)} fusion(s32[16]{0:T(128)S(1)} %multiply_add_fusion, bf16[16,40]{1,0:T(8,128)(2,1)} %param.23, s32[16]{0:T(128)} %param.21), kind=kOutput, calls=%fused_computation.21 | convolution fusion | flops 44032 | bytes 3968 | tf_op jit(solution)/shard_map/dot_general | solution.py:90
  10.9 1.4 copy.23
  12.3 1.2 all-to-all-done
  13.5 4.4 %all-to-all-start.3 = ((bf16[8,4,40]{2,1,0:T(4,128)(2,1)}), bf16[8,4,40]{2,1,0:T(4,128)(2,1)S(1)}, u32[]{:S(2)}, u32[]{:S(2)}) async-start(bf16[8,4,40]{2,1,0:T(4,128)(2,1)} %bitcast.7), calls=%async_computation.3 | async-start | bytes 16384 | tf_op jit(solution)/shard_map/all_to_all | solution.py:98
  17.9 0.6 convolution_convert_fusion.1
  18.6 1.7 %copy.24 = bf16[4,8,120,256]{3,2,1,0:T(8,128)(2,1)} copy(bf16[4,8,120,256]{3,1,2,0:T(8,128)(2,1)S(1)} %bitcast.109) | data formatting | bytes 3932160
  20.2 1.9 %all-to-all-done.3 = bf16[8,4,40]{2,1,0:T(4,128)(2,1)S(1)} async-done(((bf16[8,4,40]{2,1,0:T(4,128)(2,1)}), bf16[8,4,40]{2,1,0:T(4,128)(2,1)S(1)}, u32[]{:S(2)}, u32[]{:S(2)}) %all-to-all-start.3) | async-done | bytes 2592 | tf_op jit(solution)/shard_map/all_to_all | solution.py:98
  22.1 4.7 %all-to-all-start.1 = ((bf16[32,3,40,256]{3,2,1,0:T(8,128)(2,1)}), bf16[32,3,40,256]{3,2,1,0:T(8,128)(2,1)S(1)}, u32[]{:S(2)}, u32[]{:S(2)}) async-start(bf16[32,3,40,256]{3,2,1,0:T(8,128)(2,1)} %bitcast.108), calls=%async_computation.1 | async-start | bytes 3932160 | tf_op jit(solution)/shard_map/all_to_all | solution.py:97
  26.9 0.2 convert_reduce_fusion
  27.2 0.7 reshape.492
  27.9 43.5 %all-to-all-done.1 = bf16[32,3,40,256]{3,2,1,0:T(8,128)(2,1)S(1)} async-done(((bf16[32,3,40,256]{3,2,1,0:T(8,128)(2,1)}), bf16[32,3,40,256]{3,2,1,0:T(8,128)(2,1)S(1)}, u32[]{:S(2)}, u32[]{:S(2)}) %all-to-all-start.1) | async-done | bytes 1966112 | tf_op jit(solution)/shard_map/all_to_all | solution.py:97
  71.5 4.7 %all-to-all-start.4 = ((bf16[4,2,160]{2,1,0:T(2,128)(2,1)}), bf16[4,2,160]{2,1,0:T(2,128)(2,1)S(1)}, u32[]{:S(2)}, u32[]{:S(2)}) async-start(bf16[4,2,160]{2,1,0:T(2,128)(2,1)} %reshape.492), calls=%async_computation.4 | async-start | bytes 8192 | tf_op jit(solution)/shard_map/all_to_all | solution.py:122
  76.1 0.4 copy.25
  76.5 0.7 convolution_convert_fusion
  77.2 1.7 %copy.26 = bf16[4,8,120,256]{3,2,1,0:T(8,128)(2,1)} copy(bf16[4,8,120,256]{3,1,2,0:T(8,128)(2,1)S(1)} %bitcast.111) | data formatting | bytes 3932160
  78.9 0.4 all-to-all-done.4
  79.2 4.3 %all-to-all-start.2 = ((bf16[16,2,3,40,256]{4,3,2,1,0:T(8,128)(2,1)}), bf16[16,2,3,40,256]{4,3,2,1,0:T(8,128)(2,1)S(1)}, u32[]{:S(2)}, u32[]{:S(2)}) async-start(bf16[16,2,3,40,256]{4,3,2,1,0:T(8,128)(2,1)} %bitcast.42), calls=%async_computation.2 | async-start | bytes 3932160 | tf_op jit(solution)/shard_map/all_to_all | solution.py:121
  83.5 0.6 fusion.38
  84.1 0.6 fusion.37
  84.7 0.8 and_reduce_fusion
  85.6 21.2 %all-to-all-done.2 = bf16[16,2,3,40,256]{4,3,2,1,0:T(8,128)(2,1)S(1)} async-done(((bf16[16,2,3,40,256]{4,3,2,1,0:T(8,128)(2,1)}), bf16[16,2,3,40,256]{4,3,2,1,0:T(8,128)(2,1)S(1)}, u32[]{:S(2)}, u32[]{:S(2)}) %all-to-all-start.2) | async-done | bytes 1966112 | tf_op jit(solution)/shard_map/all_to_all | solution.py:121
  106.8 0.2 copy.19
  107.0 0.5 multiply_convert_fusion
  107.5 0.2 fusion.35
  107.7 0.2 broadcast_multiply_fusion
  107.9 0.2 fusion.36
  108.0 0.5 convolution_bitcast_fusion.5
  108.5 0.5 scatter-add.26
  109.0 1.7 %fusion.1 = f32[6,3,256,256]{3,2,0,1:T(8,128)S(1)} fusion(f32[6,3,256,256]{3,2,0,1:T(8,128)S(1)} %scatter-add.26, s32[]{:T(128)} %bitcast.16, s32[]{:T(128)} %bitcast.17, bf16[4,320,256]{2,1,0:T(8,128)(2,1)S(1)} %bitcast.101, bf16[4,320,256]{2,1,0:T(8,128)(2,1)S(1)} %bitcast.114, f32[4,1,256,256]{3,2,0,1:T(8,128)S(1)} %convolution_bitcast_fusion.5), kind=kOutput, calls=%fused_computation.12 | convolution fusion | flops 168034304 | bytes 3407880 | tf_op jit(solution)/shard_map/dot_general | solution.py:50
  110.7 2.4 %fusion.8 = f32[6,3,256,256]{3,2,0,1:T(8,128)S(1)} fusion(f32[6,3,256,256]{3,2,0,1:T(8,128)S(1)} %fusion.1, s32[]{:T(128)} %bitcast.20, s32[]{:T(128)} %bitcast.21, bf16[4,320,256]{2,1,0:T(8,128)(2,1)S(1)} %bitcast.102, bf16[4,320,256]{2,1,0:T(8,128)(2,1)S(1)} %bitcast.103, pred[]{:T(512)} %and_reduce_fusion), kind=kOutput, calls=%fused_computation.19 | convolution fusion | flops 168296448 | bytes 3407881 | tf_op jit(solution)/shard_map/dot_general | solution.py:50
  113.2 0.6 fusion.3
  113.8 0.6 fusion.5
  114.4 0.6 fusion.7
  115.1 0.2 fusion.34
  115.2 2.9 %collective-permute-start = (f32[1,3,256,256]{3,2,0,1:T(8,128)S(1)}, f32[1,3,256,256]{3,2,0,1:T(8,128)S(1)}, u32[]{:S(2)}, u32[]{:S(2)}) collective-permute-start(f32[1,3,256,256]{3,2,0,1:T(8,128)S(1)} %get-tuple-element.102), channel_id=1, source_target_pairs={{0,1},{1,2},{2,3},{3,4},{4,5},{5,6},{6,7},{7,8},{8,9},{9,10},{10,1... | collective-permute-start | bytes 2359304 | tf_op jit(solution)/shard_map/ppermute | solution.py:14
  118.1 1.9 %collective-permute-start.1 = (f32[1,3,256,256]{3,2,0,1:T(8,128)S(1)}, f32[1,3,256,256]{3,2,0,1:T(8,128)S(1)}, u32[]{:S(2)}, u32[]{:S(2)}) collective-permute-start(f32[1,3,256,256]{3,2,0,1:T(8,128)S(1)} %get-tuple-element.101), channel_id=1, source_target_pairs={{1,0},{2,1},{3,2},{4,3},{5,4},{6,5},{7,6},{8,7},{9,8},{10,9},{11,1... | collective-permute-start | bytes 2359304 | tf_op jit(solution)/shard_map/ppermute | solution.py:17
  120.1 0.2 slice.306
  120.3 15.2 %collective-permute-done = f32[1,3,256,256]{3,2,0,1:T(8,128)S(1)} collective-permute-done((f32[1,3,256,256]{3,2,0,1:T(8,128)S(1)}, f32[1,3,256,256]{3,2,0,1:T(8,128)S(1)}, u32[]{:S(2)}, u32[]{:S(2)}) %collective-permute-start) | collective-permute-done | bytes 786464 | tf_op jit(solution)/shard_map/ppermute | solution.py:14
  135.6 2.6 %collective-permute-done.1 = f32[1,3,256,256]{3,2,0,1:T(8,128)S(1)} collective-permute-done((f32[1,3,256,256]{3,2,0,1:T(8,128)S(1)}, f32[1,3,256,256]{3,2,0,1:T(8,128)S(1)}, u32[]{:S(2)}, u32[]{:S(2)}) %collective-permute-start.1) | collective-permute-done | bytes 786464 | tf_op jit(solution)/shard_map/ppermute | solution.py:17
  138.2 0.2 fusion.10
  138.3 2.1 %copy.22 = f32[4,3,256,256]{3,2,1,0:T(8,128)} copy(f32[4,3,256,256]{3,2,0,1:T(8,128)S(1)} %fusion.10) | data formatting | bytes 6291456 | tf_op jit(solution)/shard_map/scatter-add | solution.py:65
  (15 shorter events, 0.5 us)
Async XLA Ops:
  3.6 9.9 %all-to-all-start = ((bf16[8,4,1]{1,2,0:T(2,128)(2,1)}), bf16[8,4,1]{1,2,0:T(2,128)(2,1)S(1)}, u32[]{:S(2)}, u32[]{:S(2)}) async-start(bf16[8,4,1]{1,2,0:T(2,128)(2,1)} %all_to_all.48), calls=%async_computation | async-start | bytes 8192 | tf_op jit(solution)/shard_map/all_to_all | solution.py:99
  13.5 8.6 %all-to-all-start.3 = ((bf16[8,4,40]{2,1,0:T(4,128)(2,1)}), bf16[8,4,40]{2,1,0:T(4,128)(2,1)S(1)}, u32[]{:S(2)}, u32[]{:S(2)}) async-start(bf16[8,4,40]{2,1,0:T(4,128)(2,1)} %bitcast.7), calls=%async_computation.3 | async-start | bytes 16384 | tf_op jit(solution)/shard_map/all_to_all | solution.py:98
  22.1 49.3 %all-to-all-start.1 = ((bf16[32,3,40,256]{3,2,1,0:T(8,128)(2,1)}), bf16[32,3,40,256]{3,2,1,0:T(8,128)(2,1)S(1)}, u32[]{:S(2)}, u32[]{:S(2)}) async-start(bf16[32,3,40,256]{3,2,1,0:T(8,128)(2,1)} %bitcast.108), calls=%async_computation.1 | async-start | bytes 3932160 | tf_op jit(solution)/shard_map/all_to_all | solution.py:97
  71.5 7.8 %all-to-all-start.4 = ((bf16[4,2,160]{2,1,0:T(2,128)(2,1)}), bf16[4,2,160]{2,1,0:T(2,128)(2,1)S(1)}, u32[]{:S(2)}, u32[]{:S(2)}) async-start(bf16[4,2,160]{2,1,0:T(2,128)(2,1)} %reshape.492), calls=%async_computation.4 | async-start | bytes 8192 | tf_op jit(solution)/shard_map/all_to_all | solution.py:122
  77.2 7.5 %copy-start = (s32[4]{0:T(128)S(1)}, s32[4]{0:T(128)}, u32[]{:S(2)}) copy-start(s32[4]{0:T(128)} %constant.269.clone.1) | copy-start | bytes 52
  79.2 27.6 %all-to-all-start.2 = ((bf16[16,2,3,40,256]{4,3,2,1,0:T(8,128)(2,1)}), bf16[16,2,3,40,256]{4,3,2,1,0:T(8,128)(2,1)S(1)}, u32[]{:S(2)}, u32[]{:S(2)}) async-start(bf16[16,2,3,40,256]{4,3,2,1,0:T(8,128)(2,1)} %bitcast.42), calls=%async_computation.2 | async-start | bytes 3932160 | tf_op jit(solution)/shard_map/all_to_all | solution.py:121
  115.2 20.2 %collective-permute-start = (f32[1,3,256,256]{3,2,0,1:T(8,128)S(1)}, f32[1,3,256,256]{3,2,0,1:T(8,128)S(1)}, u32[]{:S(2)}, u32[]{:S(2)}) collective-permute-start(f32[1,3,256,256]{3,2,0,1:T(8,128)S(1)} %get-tuple-element.102), channel_id=1, source_target_pairs={{0,1},{1,2},{2,3},{3,4},{4,5},{5,6},{6,7},{7,8},{8,9},{9,10},{10,1... | collective-permute-start | bytes 2359304 | tf_op jit(solution)/shard_map/ppermute | solution.py:14
  118.1 20.0 %collective-permute-start.1 = (f32[1,3,256,256]{3,2,0,1:T(8,128)S(1)}, f32[1,3,256,256]{3,2,0,1:T(8,128)S(1)}, u32[]{:S(2)}, u32[]{:S(2)}) collective-permute-start(f32[1,3,256,256]{3,2,0,1:T(8,128)S(1)} %get-tuple-element.101), channel_id=1, source_target_pairs={{1,0},{2,1},{3,2},{4,3},{5,4},{6,5},{7,6},{8,7},{9,8},{10,9},{11,1... | collective-permute-start | bytes 2359304 | tf_op jit(solution)/shard_map/ppermute | solution.py:17
where the time goes:
time: 141 us; the launch traced here: 140 us
  waiting for transfers between devices  86 us (61%)
  starting transfers between devices  28.6 us (20%)
  local copies, waits for them, and re-layouts  11.3 us (8%)
  matrix products  10.2 us (7%)
  other arithmetic  4.17 us (3%)
    all_to_all x1, waiting for transfers between devices, on_device(): lax.all_to_all(packed, 'blk', split_axis=0, concat_axis=0, tiled=True)  43.5 us
    all_to_all x1, waiting for transfers between devices, on_device(): lax.all_to_all(buckets, 'rows', split_axis=0, concat_axis=1, tiled=True)  21.2 us
    ppermute x1, waiting for transfers between devices, with_halo(): lax.ppermute(lax.slice_in_dim(block, block.shape[dim] - width, None, axis...  15.2 us
    dot_general x6, matrix products, band_terms(): lax.dot_general(left, right, (((1,), (1,)), ((0,), (0,))), preferred_elem...  6.5 us
    unnamed x8, local copies, waits for them, and re-layouts  5.87 us
    all_to_all x1, starting transfers between devices, on_device(): lax.all_to_all(packed_ids, 'blk', split_axis=0, concat_axis=0, tiled=True)  5.78 us
    all_to_all x1, starting transfers between devices, on_device(): lax.all_to_all(packed, 'blk', split_axis=0, concat_axis=0, tiled=True)  4.71 us
    all_to_all x1, starting transfers between devices, on_device(): lax.all_to_all(bucket_wts, 'rows', split_axis=0, concat_axis=1, tiled=True)  4.67 us
  transfers between devices with their start and end apart: 7, of which 7 were waited for; matrix products, arithmetic and copies ran while one was open for 8% of the time, Pallas kernels for 0%

commit v1 on v0

--- a/solution.py
+++ b/solution.py
@@ -4,6 +4,25 @@
 from jax.sharding import PartitionSpec as P
 
 KB = 16
+
+
+def _step_on_run(which_dim, array_axis, state):
+    named_axis = "rows"
+    all_rows = jax.lax.axis_size(named_axis)
+    z = jax.lax.axis_index(named_axis)
+    arr_out, x_new = (all_rows, z)
+    vec_out = state.shape[array_axis] // arr_out
+    w1 = jnp.roll(state, -x_new * vec_out, axis=array_axis)
+    vals = [lax.slice_in_dim(w1, 0, vec_out, axis=array_axis)]
+    for hop_no in range(1, arr_out):
+        finding = lax.slice_in_dim(w1, hop_no * vec_out, (hop_no + 1) * vec_out, axis=array_axis)
+        small = jax.lax.ppermute(
+            finding, named_axis, [(src_i, (src_i + hop_no) % arr_out) for src_i in range(arr_out)]
+        )
+        vals.append(small)
+    formed = jnp.concatenate(vals[::-1], axis=which_dim)
+    step_out = jnp.roll(formed, shift=(x_new + 1) * vals[0].shape[which_dim], axis=which_dim)
+    return step_out
 
 
 def with_halo(block, sides, width):
@@ -118,7 +137,7 @@
     mine_blk = lax.axis_index("blk")
     share = KB // lax.axis_size("rows")
     moved, moved_wts = (
-        lax.all_to_all(buckets, "rows", split_axis=0, concat_axis=1, tiled=True),
+        _step_on_run(1, 0, buckets),
         lax.all_to_all(bucket_wts, "rows", split_axis=0, concat_axis=1, tiled=True),
     )
     base = mine_blk * KB + lax.axis_index("rows") * share

time: 141 us -> 131 us (0.929)
  waiting for transfers between devices: 86 us -> 75.9 us
    all_to_all x1 -> x0, waiting for transfers between devices: 21.2 us -> none  [on_device(): lax.all_to_all(buckets, 'rows', split_axis=0, concat_axis=1, tiled=True)]
    all_to_all x1, waiting for transfers between devices: 0.38 us -> 16 us  [on_device(): lax.all_to_all(bucket_wts, 'rows', split_axis=0, concat_axis=1, tiled=True)]
    all_to_all x1 -> x0, starting transfers between devices: 4.27 us -> none  [on_device(): lax.all_to_all(buckets, 'rows', split_axis=0, concat_axis=1, tiled=True)]
    ppermute x0 -> x3, starting transfers between devices: none -> 3.93 us  [_step_on_run(): jax.lax.ppermute(finding, named_axis, [(src_i, (src_i + hop_no) % arr_out...]
    all_to_all x1, waiting for transfers between devices: 1.91 us -> 0.01 us  [on_device(): lax.all_to_all(packed_wts, 'blk', split_axis=0, concat_axis=0, tiled=True)]
    unnamed x8 -> x19, local copies, waits for them, and re-layouts: 5.87 us -> 4.85 us
  transfers between devices with their start and end apart: 7 -> 9, of which waited for: 7 -> 5; matrix products, arithmetic and copies ran while one was open for 8% -> 9% of each run, Pallas kernels for 0% -> 0%
where the time goes in v1:
time: 131 us; the launch traced here: 130 us
  waiting for transfers between devices  75.9 us (58%)
  starting transfers between devices  27.7 us (21%)
  local copies, waits for them, and re-layouts  11.2 us (9%)
  matrix products  9.47 us (7%)
  other arithmetic  4.94 us (4%)
    all_to_all x1, waiting for transfers between devices, on_device(): lax.all_to_all(packed, 'blk', split_axis=0, concat_axis=0, tiled=True)  42.2 us
    all_to_all x1, waiting for transfers between devices, on_device(): lax.all_to_all(bucket_wts, 'rows', split_axis=0, concat_axis=1, tiled=True)  16 us
    ppermute x1, waiting for transfers between devices, with_halo(): lax.ppermute(lax.slice_in_dim(block, block.shape[dim] - width, None, axis...  15.2 us
    dot_general x6, matrix products, band_terms(): lax.dot_general(left, right, (((1,), (1,)), ((0,), (0,))), preferred_elem...  6.49 us
    all_to_all x1, starting transfers between devices, on_device(): lax.all_to_all(packed_ids, 'blk', split_axis=0, concat_axis=0, tiled=True)  5.78 us
    all_to_all x1, starting transfers between devices, on_device(): lax.all_to_all(packed, 'blk', split_axis=0, concat_axis=0, tiled=True)  5.03 us
    unnamed x19, local copies, waits for them, and re-layouts  4.85 us
    all_to_all x1, starting transfers between devices, on_device(): lax.all_to_all(packed_wts, 'blk', split_axis=0, concat_axis=0, tiled=True)  4.54 us
  transfers between devices with their start and end apart: 9, of which 5 were waited for; matrix products, arithmetic and copies ran while one was open for 9% of the time, Pallas kernels for 0%

profile of v1, /device:TPU:3, one launch (start us, length us, event | category | flops | bytes accessed | tf_op | source)
XLA Modules:
  0.0 129.5 jit_solution(14508968408892559565)
XLA Ops:
  0.0 0.7 and_select_fusion.1
  0.7 0.7 fusion.57
  1.3 0.2 convert_reduce_fusion.1
  1.5 0.7 multiply_add_fusion
  2.2 0.8 fusion.10
  3.0 0.7 all_to_all.31
  3.6 5.8 %all-to-all-start = ((bf16[8,4,1]{1,2,0:T(2,128)(2,1)}), bf16[8,4,1]{1,2,0:T(2,128)(2,1)S(1)}, u32[]{:S(2)}, u32[]{:S(2)}) async-start(bf16[8,4,1]{1,2,0:T(2,128)(2,1)} %all_to_all.31), calls=%async_computation | async-start | bytes 8192 | tf_op jit(solution)/shard_map/all_to_all | solution.py:118
  9.4 1.4 %copy.15 = bf16[2,8,120,256]{3,1,2,0:T(8,128)(2,1)S(1)} copy(bf16[2,8,120,256]{3,2,1,0:T(8,128)(2,1)} %bitcast.113) | data formatting | bytes 1966080
  10.8 0.6 convolution_convert_fusion.1
  11.5 1.7 %copy.16 = bf16[4,8,120,256]{3,2,1,0:T(8,128)(2,1)} copy(bf16[4,8,120,256]{3,1,2,0:T(8,128)(2,1)S(1)} %bitcast.103) | data formatting | bytes 3932160
  13.2 0.4 all-to-all-done
  13.6 5.0 %all-to-all-start.1 = ((bf16[32,3,40,256]{3,2,1,0:T(8,128)(2,1)}), bf16[32,3,40,256]{3,2,1,0:T(8,128)(2,1)S(1)}, u32[]{:S(2)}, u32[]{:S(2)}) async-start(bf16[32,3,40,256]{3,2,1,0:T(8,128)(2,1)} %bitcast.101), calls=%async_computation.1 | async-start | bytes 3932160 | tf_op jit(solution)/shard_map/all_to_all | solution.py:116
  18.6 0.6 fusion.39
  19.2 0.7 and_reduce_fusion
  20.0 0.8 convolution_convert_fusion.3
  20.9 0.2 convert_reduce_fusion
  21.1 42.2 %all-to-all-done.1 = bf16[32,3,40,256]{3,2,1,0:T(8,128)(2,1)S(1)} async-done(((bf16[32,3,40,256]{3,2,1,0:T(8,128)(2,1)}), bf16[32,3,40,256]{3,2,1,0:T(8,128)(2,1)S(1)}, u32[]{:S(2)}, u32[]{:S(2)}) %all-to-all-start.1) | async-done | bytes 1966112 | tf_op jit(solution)/shard_map/all_to_all | solution.py:116
  63.3 4.5 %all-to-all-start.2 = ((bf16[8,4,40]{2,1,0:T(4,128)(2,1)}), bf16[8,4,40]{2,1,0:T(4,128)(2,1)S(1)}, u32[]{:S(2)}, u32[]{:S(2)}) async-start(bf16[8,4,40]{2,1,0:T(4,128)(2,1)} %bitcast.4), calls=%async_computation.2 | async-start | bytes 16384 | tf_op jit(solution)/shard_map/all_to_all | solution.py:117
  67.8 0.4 copy.17
  68.2 0.7 convolution_convert_fusion
  68.9 0.4 copy.18
  69.3 0.7 fusion
  70.0 1.1 fusion.38
  71.2 1.1 collective-permute-start
  72.2 1.2 collective-permute-start.1
  73.6 0.7 reshape.492
  74.3 3.7 %all-to-all-start.3 = ((bf16[4,2,160]{2,1,0:T(2,128)(2,1)}), bf16[4,2,160]{2,1,0:T(2,128)(2,1)S(1)}, u32[]{:S(2)}, u32[]{:S(2)}) async-start(bf16[4,2,160]{2,1,0:T(2,128)(2,1)} %reshape.492), calls=%async_computation.3 | async-start | bytes 8192 | tf_op jit(solution)/shard_map/all_to_all | solution.py:141
  77.9 1.6 %collective-permute-start.2 = (bf16[4,2,3,40,256]{4,3,2,1,0:T(8,128)(2,1)}, bf16[4,2,3,40,256]{4,3,2,1,0:T(8,128)(2,1)S(1)}, u32[]{:S(2)}, u32[]{:S(2)}) collective-permute-start(bf16[4,2,3,40,256]{4,3,2,1,0:T(8,128)(2,1)} %get-tuple-element.109), channel_id=1, source_target_pairs={{0,1},{1,2},{2,3},{3,0},{4,5},{5,6},{6,7},{7,4},{8,9},{9,10},{10,1... | collective-permute-start | bytes 1474568 | tf_op jit(solution)/shard_map/ppermute | solution.py:19
  79.6 0.6 fusion.40
  80.2 16.0 %all-to-all-done.3 = bf16[4,2,160]{2,1,0:T(2,128)(2,1)S(1)} async-done(((bf16[4,2,160]{2,1,0:T(2,128)(2,1)}), bf16[4,2,160]{2,1,0:T(2,128)(2,1)S(1)}, u32[]{:S(2)}, u32[]{:S(2)}) %all-to-all-start.3) | async-done | bytes 2592 | tf_op jit(solution)/shard_map/all_to_all | solution.py:141
  96.6 0.2 dynamic-slice_multiply_fusion
  96.8 0.2 fusion.37
  97.0 0.5 multiply_convert_fusion
  97.5 0.2 fusion.36
  97.7 0.5 convolution_bitcast_fusion.5
  98.2 0.5 scatter-add.26
  98.7 1.7 %fusion.2 = f32[6,3,256,256]{3,2,0,1:T(8,128)S(1)} fusion(f32[6,3,256,256]{3,2,0,1:T(8,128)S(1)} %scatter-add.26, s32[]{:T(128)} %bitcast.13, s32[]{:T(128)} %bitcast.14, bf16[4,320,256]{2,1,0:T(8,128)(2,1)S(1)} %bitcast.95, bf16[4,320,256]{2,1,0:T(8,128)(2,1)S(1)} %bitcast.106, f32[4,1,256,256]{3,2,0,1:T(8,128)S(1)} %convolution_bitcast_fusion.5), kind=kOutput, calls=%fused_computation.16 | convolution fusion | flops 168034304 | bytes 3407880 | tf_op jit(solution)/shard_map/dot_general | solution.py:69
  100.4 2.4 %fusion.9 = f32[6,3,256,256]{3,2,0,1:T(8,128)S(1)} fusion(f32[6,3,256,256]{3,2,0,1:T(8,128)S(1)} %fusion.2, s32[]{:T(128)} %bitcast.17, s32[]{:T(128)} %bitcast.18, bf16[4,320,256]{2,1,0:T(8,128)(2,1)S(1)} %bitcast.96, bf16[4,320,256]{2,1,0:T(8,128)(2,1)S(1)} %bitcast.97, pred[]{:T(512)} %and_reduce_fusion), kind=kOutput, calls=%fused_computation.23 | convolution fusion | flops 168296448 | bytes 3407881 | tf_op jit(solution)/shard_map/dot_general | solution.py:69
  102.9 0.6 fusion.4
  103.5 0.6 fusion.6
  104.1 0.6 fusion.8
  104.7 0.2 fusion.35
  104.9 2.8 %collective-permute-start.3 = (f32[1,3,256,256]{3,2,0,1:T(8,128)S(1)}, f32[1,3,256,256]{3,2,0,1:T(8,128)S(1)}, u32[]{:S(2)}, u32[]{:S(2)}) collective-permute-start(f32[1,3,256,256]{3,2,0,1:T(8,128)S(1)} %get-tuple-element.102), channel_id=1, source_target_pairs={{0,1},{1,2},{2,3},{3,4},{4,5},{5,6},{6,7},{7,8},{8,9},{9,10},{10,1... | collective-permute-start | bytes 2359304 | tf_op jit(solution)/shard_map/ppermute | solution.py:33
  107.8 1.9 %collective-permute-start.4 = (f32[1,3,256,256]{3,2,0,1:T(8,128)S(1)}, f32[1,3,256,256]{3,2,0,1:T(8,128)S(1)}, u32[]{:S(2)}, u32[]{:S(2)}) collective-permute-start(f32[1,3,256,256]{3,2,0,1:T(8,128)S(1)} %get-tuple-element.101), channel_id=1, source_target_pairs={{1,0},{2,1},{3,2},{4,3},{5,4},{6,5},{7,6},{8,7},{9,8},{10,9},{11,1... | collective-permute-start | bytes 2359304 | tf_op jit(solution)/shard_map/ppermute | solution.py:36
  109.7 0.2 slice.326
  109.9 15.2 %collective-permute-done.3 = f32[1,3,256,256]{3,2,0,1:T(8,128)S(1)} collective-permute-done((f32[1,3,256,256]{3,2,0,1:T(8,128)S(1)}, f32[1,3,256,256]{3,2,0,1:T(8,128)S(1)}, u32[]{:S(2)}, u32[]{:S(2)}) %collective-permute-start.3) | collective-permute-done | bytes 786464 | tf_op jit(solution)/shard_map/ppermute | solution.py:33
  125.2 2.1 %collective-permute-done.4 = f32[1,3,256,256]{3,2,0,1:T(8,128)S(1)} collective-permute-done((f32[1,3,256,256]{3,2,0,1:T(8,128)S(1)}, f32[1,3,256,256]{3,2,0,1:T(8,128)S(1)}, u32[]{:S(2)}, u32[]{:S(2)}) %collective-permute-start.4) | collective-permute-done | bytes 786464 | tf_op jit(solution)/shard_map/ppermute | solution.py:36
  127.5 2.1 %copy.14 = f32[4,3,256,256]{3,2,1,0:T(8,128)} copy(f32[4,3,256,256]{3,2,0,1:T(8,128)S(1)} %fusion.11) | data formatting | bytes 6291456 | tf_op jit(solution)/shard_map/scatter-add | solution.py:84
  (31 shorter events, 1.0 us)
Async XLA Ops:
  3.6 9.9 %all-to-all-start = ((bf16[8,4,1]{1,2,0:T(2,128)(2,1)}), bf16[8,4,1]{1,2,0:T(2,128)(2,1)S(1)}, u32[]{:S(2)}, u32[]{:S(2)}) async-start(bf16[8,4,1]{1,2,0:T(2,128)(2,1)} %all_to_all.31), calls=%async_computation | async-start | bytes 8192 | tf_op jit(solution)/shard_map/all_to_all | solution.py:118
  11.5 7.7 %copy-start = (s32[4]{0:T(128)S(1)}, s32[4]{0:T(128)}, u32[]{:S(2)}) copy-start(s32[4]{0:T(128)} %constant.309.clone.1) | copy-start | bytes 52
  11.5 8.5 %copy-start.1 = (bf16[16,40]{1,0:T(8,128)(2,1)S(1)}, bf16[16,40]{1,0:T(8,128)(2,1)}, u32[]{:S(2)}) copy-start(bf16[16,40]{1,0:T(8,128)(2,1)} %param.23) | copy-start | bytes 3844
  11.5 8.5 %copy-start.2 = (s32[16]{0:T(128)S(1)}, s32[16]{0:T(128)}, u32[]{:S(2)}) copy-start(s32[16]{0:T(128)} %param.21) | copy-start | bytes 196
  13.6 49.7 %all-to-all-start.1 = ((bf16[32,3,40,256]{3,2,1,0:T(8,128)(2,1)}), bf16[32,3,40,256]{3,2,1,0:T(8,128)(2,1)S(1)}, u32[]{:S(2)}, u32[]{:S(2)}) async-start(bf16[32,3,40,256]{3,2,1,0:T(8,128)(2,1)} %bitcast.101), calls=%async_computation.1 | async-start | bytes 3932160 | tf_op jit(solution)/shard_map/all_to_all | solution.py:116
  63.3 10.1 %all-to-all-start.2 = ((bf16[8,4,40]{2,1,0:T(4,128)(2,1)}), bf16[8,4,40]{2,1,0:T(4,128)(2,1)S(1)}, u32[]{:S(2)}, u32[]{:S(2)}) async-start(bf16[8,4,40]{2,1,0:T(4,128)(2,1)} %bitcast.4), calls=%async_computation.2 | async-start | bytes 16384 | tf_op jit(solution)/shard_map/all_to_all | solution.py:117
  71.2 25.1 %collective-permute-start = (bf16[4,2,3,40,256]{4,3,2,1,0:T(8,128)(2,1)}, bf16[4,2,3,40,256]{4,3,2,1,0:T(8,128)(2,1)S(1)}, u32[]{:S(2)}, u32[]{:S(2)}) collective-permute-start(bf16[4,2,3,40,256]{4,3,2,1,0:T(8,128)(2,1)} %get-tuple-element.111), channel_id=1, source_target_pairs={{0,3},{1,0},{2,1},{3,2},{4,7},{5,4},{6,5},{7,6},{8,11},{9,8},{10,9... | collective-permute-start | bytes 1474568 | tf_op jit(solution)/shard_map/ppermute | solution.py:19
  72.2 24.1 %collective-permute-start.1 = (bf16[4,2,3,40,256]{4,3,2,1,0:T(8,128)(2,1)}, bf16[4,2,3,40,256]{4,3,2,1,0:T(8,128)(2,1)S(1)}, u32[]{:S(2)}, u32[]{:S(2)}) collective-permute-start(bf16[4,2,3,40,256]{4,3,2,1,0:T(8,128)(2,1)} %get-tuple-element.110), channel_id=1, source_target_pairs={{0,2},{1,3},{2,0},{3,1},{4,6},{5,7},{6,4},{7,5},{8,10},{9,11},{10,... | collective-permute-start | bytes 1474568 | tf_op jit(solution)/shard_map/ppermute | solution.py:19
  74.3 21.9 %all-to-all-start.3 = ((bf16[4,2,160]{2,1,0:T(2,128)(2,1)}), bf16[4,2,160]{2,1,0:T(2,128)(2,1)S(1)}, u32[]{:S(2)}, u32[]{:S(2)}) async-start(bf16[4,2,160]{2,1,0:T(2,128)(2,1)} %reshape.492), calls=%async_computation.3 | async-start | bytes 8192 | tf_op jit(solution)/shard_map/all_to_all | solution.py:141
  77.9 18.4 %collective-permute-start.2 = (bf16[4,2,3,40,256]{4,3,2,1,0:T(8,128)(2,1)}, bf16[4,2,3,40,256]{4,3,2,1,0:T(8,128)(2,1)S(1)}, u32[]{:S(2)}, u32[]{:S(2)}) collective-permute-start(bf16[4,2,3,40,256]{4,3,2,1,0:T(8,128)(2,1)} %get-tuple-element.109), channel_id=1, source_target_pairs={{0,1},{1,2},{2,3},{3,0},{4,5},{5,6},{6,7},{7,4},{8,9},{9,10},{10,1... | collective-permute-start | bytes 1474568 | tf_op jit(solution)/shard_map/ppermute | solution.py:19
  104.9 20.2 %collective-permute-start.3 = (f32[1,3,256,256]{3,2,0,1:T(8,128)S(1)}, f32[1,3,256,256]{3,2,0,1:T(8,128)S(1)}, u32[]{:S(2)}, u32[]{:S(2)}) collective-permute-start(f32[1,3,256,256]{3,2,0,1:T(8,128)S(1)} %get-tuple-element.102), channel_id=1, source_target_pairs={{0,1},{1,2},{2,3},{3,4},{4,5},{5,6},{6,7},{7,8},{8,9},{9,10},{10,1... | collective-permute-start | bytes 2359304 | tf_op jit(solution)/shard_map/ppermute | solution.py:33
  107.8 19.5 %collective-permute-start.4 = (f32[1,3,256,256]{3,2,0,1:T(8,128)S(1)}, f32[1,3,256,256]{3,2,0,1:T(8,128)S(1)}, u32[]{:S(2)}, u32[]{:S(2)}) collective-permute-start(f32[1,3,256,256]{3,2,0,1:T(8,128)S(1)} %get-tuple-element.101), channel_id=1, source_target_pairs={{1,0},{2,1},{3,2},{4,3},{5,4},{6,5},{7,6},{8,7},{9,8},{10,9},{11,1... | collective-permute-start | bytes 2359304 | tf_op jit(solution)/shard_map/ppermute | solution.py:36
